TPU v7x, 32 devices: a whole 2x2x4 slice. The times are simulated.
32 devices in a mesh: row: 2 (over x), col: 16 (over z, y, core).
Axes of the slice: x: 2, y: 2, z: 4, core: 2. Of those that a mesh axis runs over, the one named last changes fastest.
Arguments:
- upper_a: float32 [8, 2, 256, 16, 256], P(None, 'row', None, 'col'), may hold values from -0.375 to 0.375
- upper_b: float32 [8, 2, 256, 16, 256], P(None, 'row', None, 'col'), may hold values from -0.375 to 0.375
- right_side: float32 [8, 2, 256, 16, 256], P(None, 'row', None, 'col'), may hold values from -6 to 6
- vectors_a: float32 [8, 2, 256, 256], P(None, 'row'), may hold values from -0.375 to 0.375
- inverse_a: float32 [8, 2, 256, 256], P(None, 'row'), may hold values from -0.375 to 0.375
- values_a: float32 [8, 2, 256], P(None, 'row'), may hold values from 0.5 to 2
- vectors_b: float32 [16, 256, 256], P('col'), may hold values from -0.375 to 0.375
- inverse_b: float32 [16, 256, 256], P('col'), may hold values from -0.375 to 0.375
- values_b: float32 [16, 256], P('col'), may hold values from 0.5 to 2
Outputs:
- solved: float32 [8, 2, 256, 16, 256], P(None, 'row', None, 'col')
All inputs are finite; a program needn't handle non-finite values.
Results may differ from a plain program's by a relative error of at most 0.0001.
Values sent between devices are 32-bit elements; how exact they have to be, the bound alone decides.
A program may use at most 64 MiB of HBM per device.

v0:
```python
import jax
import jax.numpy as jnp
from jax import lax
from jax.sharding import PartitionSpec as P

FRONTS = 4
EXACT = lax.Precision.HIGHEST


def passed_along(value, axis, by):
    length = lax.axis_size(axis)
    pairs = [(i, i + by) for i in range(length) if 0 <= i + by < length]
    return lax.ppermute(value, axis, pairs)


def shifted(value, axis, steps):
    count = lax.axis_size(axis)
    pairs = [(source, (source + steps) % count) for source in range(count)]
    return lax.ppermute(value, axis, pairs)


def spread(value, axis, root):
    mine = lax.axis_index(axis) == root
    return lax.psum(jnp.where(mine, value, jnp.zeros_like(value)), axis)


def matmul(former, latter):
    return jnp.dot(former, latter, precision=EXACT, preferred_element_type=jnp.float32)


def diagonal_solve(residual, vectors_a, inverse_a, values_a, vectors_b, inverse_b, values_b):
    rotated = matmul(matmul(inverse_a, residual), vectors_b)
    scaled = rotated / (values_a[:, None] + values_b[None, :])
    return matmul(matmul(vectors_a, scaled), inverse_b)


def body(
    upper_a, upper_b, right_side, vectors_a, inverse_a, values_a, vectors_b, inverse_b, values_b
):
    row_count = lax.axis_size("row")
    col_count = lax.axis_size("col")
    row_pos = lax.axis_index("row")
    col_pos = lax.axis_index("col")
    local_blocks = right_side.shape[0]
    block_size = right_side.shape[2]
    square = (local_blocks, block_size, block_size)
    panel_a = upper_a.reshape(square)
    panel_b = upper_b.reshape(square)
    work = right_side.reshape(square)
    left_vectors = vectors_a.reshape(square)
    left_inverse = inverse_a.reshape(square)
    left_values = values_a.reshape(local_blocks, block_size)
    right_vectors = vectors_b.reshape(block_size, block_size)
    right_inverse = inverse_b.reshape(block_size, block_size)
    right_values = values_b.reshape(block_size)
    block_ids = jnp.arange(local_blocks, dtype=jnp.int32)
    global_rows = block_ids * row_count + row_pos
    offsets = list(range(-1, FRONTS - 1))
    moved_upper = {}
    for offset in offsets:
        if offset == 0:
            moved_upper[offset] = panel_a
        else:
            moved_upper[offset] = passed_along(panel_a, "col", offset)
    zero_block = jnp.zeros((1, block_size, block_size), jnp.float32)
    moved_lower = {}
    for offset in offsets:
        if offset % row_count == 0:
            arrived = panel_b
        else:
            arrived = shifted(panel_b, "row", -offset)
        block_carry = jnp.floor_divide(row_pos + offset, row_count)
        padded = jnp.concatenate([zero_block, arrived, zero_block], axis=0)
        moved_lower[offset] = lax.dynamic_slice_in_dim(padded, 1 + block_carry, local_blocks, 0)
    for offset in offsets:
        target = col_pos - offset
        slot_index = jnp.floor_divide(target - row_pos, row_count)
        present = (
            (jnp.remainder(target - row_pos, row_count) == 0) & (target >= 0) & (target < col_count)
        )
        picked = jnp.clip(slot_index, 0, local_blocks - 1)
        residual = lax.dynamic_index_in_dim(work, picked, 0, keepdims=False)
        solved = diagonal_solve(
            residual,
            lax.dynamic_index_in_dim(left_vectors, picked, 0, keepdims=False),
            lax.dynamic_index_in_dim(left_inverse, picked, 0, keepdims=False),
            lax.dynamic_index_in_dim(left_values, picked, 0, keepdims=False),
            right_vectors,
            right_inverse,
            right_values,
        )
        on_front = (block_ids == slot_index) & present
        work = jnp.where(on_front[:, None, None], solved[None], work)
        column_block = spread(solved, "row", jnp.remainder(target, row_count))
        upper_term = jnp.einsum("qab,bc->qac", moved_upper[offset], column_block, precision=EXACT)
        slot_blocks = jnp.where(on_front[:, None, None], solved[None], jnp.zeros_like(work))
        row_solved = lax.psum(slot_blocks, "col")
        lower_term = jnp.einsum("qab,qbc->qac", row_solved, moved_lower[offset], precision=EXACT)
        pending = col_pos - global_rows > offset
        work = jnp.where(pending[:, None, None], work - (upper_term + lower_term), work)
    return work.reshape(right_side.shape)


def solution(mesh):
    return jax.shard_map(
        body,
        mesh=mesh,
        in_specs=(
            P(None, "row", None, "col", None),
            P(None, "row", None, "col", None),
            P(None, "row", None, "col", None),
            P(None, "row", None, None),
            P(None, "row", None, None),
            P(None, "row", None),
            P("col", None, None),
            P("col", None, None),
            P("col", None),
        ),
        out_specs=P(None, "row", None, "col", None),
        check_vma=False,
    )
```

profile of v0, /device:TPU:0, one launch (start us, length us, event | category | flops | bytes accessed | tf_op | source)
XLA Modules:
  0.0 592.5 jit_solution(1330975827765755095)
XLA Ops:
  6.5 3.2 copy.54
  9.7 3.0 collective-permute-start.1
  12.7 1.5 copy.55
  14.3 1.4 collective-permute-start
  20.5 1.7 broadcast_select_fusion.3
  22.5 6.0 %copy.11 = f32[8,1,256,1,256]{2,4,0,3,1:T(8,128)} copy(f32[8,1,256,1,256]{4,3,2,1,0:T(1,128)} %param.11) | data formatting | bytes 4194304 | tf_op args[2]
  28.6 35.7 %collective-permute-done.1 = f32[8,256,256]{2,1,0:T(8,128)} collective-permute-done((f32[8,256,256]{2,1,0:T(8,128)}, f32[8,256,256]{2,1,0:T(8,128)}, u32[]{:S(2)}, u32[]{:S(2)}) %collective-permute-start.1) | collective-permute-done | bytes 2097184 | tf_op jit(solution)/shard_map/ppermute | solution.py:19
  64.3 5.4 pad_maximum_fusion
  69.7 6.5 %fusion.26 = f32[256,8,256]{2,0,1:T(8,128)} fusion(f32[8,256,256]{2,1,0:T(8,128)} %collective-permute-done, f32[256,256]{1,0:T(8,128)} %all-reduce.9.cloned.1.call-done), kind=kOutput, calls=%fused_computation.45 | convolution fusion | flops 1610612736 | bytes 4456448 | tf_op jit(solution)/shard_map/qab,bc->qac/dot_general | solution.py:95
  76.2 77.0 %all-reduce.11.cloned.1.call-done = f32[8,256,256]{1,2,0:T(8,128)} async-done(((f32[8,256,256]{1,2,0:T(8,128)}), f32[8,256,256]{1,2,0:T(8,128)}) %all-reduce.11.cloned.1.call-update) | async-done | bytes 2097168 | tf_op jit(solution)/shard_map/psum | solution.py:97
  153.2 7.2 %subtract_select_fusion.3 = f32[8,256,256]{1,2,0:T(8,128)S(1)} fusion(f32[256,8,256]{2,0,1:T(8,128)} %fusion.26, f32[8,1,256,1,256]{2,4,0,3,1:T(8,128)} %copy.11, f32[8,256,256]{1,2,0:T(8,128)} %all-reduce.11.cloned.1.call-done, f32[10,256,256]{2,1,0:T(8,128)} %get-tuple-element.8, s32[]{:T(128)S(6)} %select_n.168, f32[256,256]{0,1:T(8,128)S(1)} %copy.10, ...), kind=kOutput, calls=%fused_computation.7 | convolution fusion | flops 1612709888 | bytes 10747924 | tf_op jit(solution)/shard_map/qab,qbc->qac/dot_general | solution.py:98
  160.4 1.3 copy-done.2
  162.5 1.3 fusion.44
  165.1 1.7 broadcast_select_fusion.2
  166.9 2.7 collective-permute-start.2
  170.2 98.3 %all-reduce.15.cloned.1.call-done = f32[8,256,256]{1,2,0:T(8,128)} async-done(((f32[8,256,256]{1,2,0:T(8,128)}), f32[8,256,256]{1,2,0:T(8,128)}) %all-reduce.15.cloned.1.call-update) | async-done | bytes 2097168 | tf_op jit(solution)/shard_map/psum | solution.py:97
  268.5 7.2 %fusion.5 = f32[8,256,256]{1,2,0:T(8,128)} fusion(f32[8,256,256]{1,2,0:T(8,128)} %all-reduce.15.cloned.1.call-done, f32[10,256,256]{2,1,0:T(8,128)} %get-tuple-element.7, s32[]{:T(128)S(6)} %select_n.176), kind=kOutput, calls=%fused_computation.20 | convolution fusion | flops 1610612736 | bytes 6291460 | tf_op jit(solution)/shard_map/qab,qbc->qac/dot_general | solution.py:98
  275.7 17.7 %all-reduce.13.cloned.1.call-done = f32[256,256]{1,0:T(8,128)} async-done(((f32[256,256]{1,0:T(8,128)}), f32[256,256]{1,0:T(8,128)}) %all-reduce.13.cloned.1.call-update) | async-done | bytes 262160 | tf_op jit(solution)/shard_map/psum | solution.py:24
  293.4 6.7 %subtract_select_fusion.2 = f32[8,256,256]{1,2,0:T(8,128)S(1)} fusion(f32[8,256,256]{1,2,0:T(8,128)} %fusion.5, f32[8,256,256]{1,2,0:T(8,128)} %copy-done.2, f32[256,256]{0,1:T(8,128)S(1)} %copy.15, pred[8]{0:T(512)(128)(4,1)S(1)} %compare_and_fusion.1, pred[8]{0:T(512)(128)(4,1)S(1)} %get-tuple-element.14, f32[256,256]{1,0:T(8,128)} %all-reduce.13.cloned.1.call-done, ...), kind=kOutput, calls=%fused_computation.6 | convolution fusion | flops 1612709888 | bytes 8912912 | tf_op jit(solution)/shard_map/qab,bc->qac/dot_general | solution.py:95
  304.9 1.6 broadcast_select_fusion.1
  306.5 4.9 collective-permute-start.3
  311.5 16.8 %all-reduce.17.cloned.1.call-done = f32[256,256]{1,0:T(8,128)} async-done(((f32[256,256]{1,0:T(8,128)}), f32[256,256]{1,0:T(8,128)}) %all-reduce.17.cloned.1.call-update) | async-done | bytes 262160 | tf_op jit(solution)/shard_map/psum | solution.py:24
  328.3 6.5 %fusion.19 = f32[256,8,256]{2,0,1:T(8,128)} fusion(f32[8,256,256]{2,1,0:T(8,128)} %collective-permute-done.2, f32[256,256]{1,0:T(8,128)} %all-reduce.17.cloned.1.call-done), kind=kOutput, calls=%fused_computation.38 | convolution fusion | flops 1610612736 | bytes 4456448 | tf_op jit(solution)/shard_map/qab,bc->qac/dot_general | solution.py:95
  334.8 100.3 %all-reduce.19.cloned.1.call-done = f32[8,256,256]{1,2,0:T(8,128)} async-done(((f32[8,256,256]{1,2,0:T(8,128)}), f32[8,256,256]{1,2,0:T(8,128)}) %all-reduce.19.cloned.1.call-update) | async-done | bytes 2097168 | tf_op jit(solution)/shard_map/psum | solution.py:97
  435.1 7.2 %subtract_select_fusion.1 = f32[8,256,256]{1,2,0:T(8,128)S(1)} fusion(f32[256,8,256]{2,0,1:T(8,128)} %fusion.19, f32[8,256,256]{1,2,0:T(8,128)} %copy-done.1, f32[8,256,256]{1,2,0:T(8,128)} %all-reduce.19.cloned.1.call-done, f32[10,256,256]{2,1,0:T(8,128)} %get-tuple-element.8, s32[]{:T(128)S(6)} %select_n.184, f32[256,256]{0,1:T(8,128)S(1)} %copy.19, ...), kind=kOutput, calls=%fused_computation.5 | convolution fusion | flops 1612709888 | bytes 10747924 | tf_op jit(solution)/shard_map/qab,qbc->qac/dot_general | solution.py:98
  442.3 1.3 copy-done.3
  447.0 1.5 broadcast_select_fusion
  449.3 97.0 %all-reduce.23.cloned.1.call-done = f32[8,256,256]{1,2,0:T(8,128)} async-done(((f32[8,256,256]{1,2,0:T(8,128)}), f32[8,256,256]{1,2,0:T(8,128)}) %all-reduce.23.cloned.1.call-update) | async-done | bytes 2097168 | tf_op jit(solution)/shard_map/psum | solution.py:97
  546.4 7.0 %fusion.1 = f32[8,256,256]{1,2,0:T(8,128)} fusion(f32[8,256,256]{1,2,0:T(8,128)} %all-reduce.23.cloned.1.call-done, f32[10,256,256]{2,1,0:T(8,128)} %get-tuple-element.7, s32[]{:T(128)S(6)} %select_n.192), kind=kOutput, calls=%fused_computation.16 | convolution fusion | flops 1610612736 | bytes 6291460 | tf_op jit(solution)/shard_map/qab,qbc->qac/dot_general | solution.py:98
  553.4 18.0 %all-reduce.21.cloned.1.call-done = f32[256,256]{1,0:T(8,128)} async-done(((f32[256,256]{1,0:T(8,128)}), f32[256,256]{1,0:T(8,128)}) %all-reduce.21.cloned.1.call-update) | async-done | bytes 262160 | tf_op jit(solution)/shard_map/psum | solution.py:24
  571.5 8.0 %fusion = f32[8,1,256,1,256]{2,4,0,3,1:T(8,128)} fusion(f32[8,256,256]{1,2,0:T(8,128)} %fusion.1, f32[8,256,256]{1,2,0:T(8,128)} %copy-done.3, f32[8,256,256]{2,1,0:T(8,128)} %collective-permute-done.3, f32[256,256]{0,1:T(8,128)S(1)} %copy.23, pred[8]{0:T(512)(128)(4,1)S(1)} %compare_and_fusion.3, pred[8]{0:T(512)(128)(4,1)S(1)} %get-tuple-element.5, ...), kind=kOutput, calls=%fused_computation.8 | convolution fusion | flops 1612709888 | bytes 8912912 | tf_op jit(solution)/shard_map/qab,bc->qac/dot_general | solution.py:95
  579.4 6.0 %copy.27 = f32[8,1,256,1,256]{4,3,2,1,0:T(1,128)} copy(f32[8,1,256,1,256]{2,4,0,3,1:T(8,128)} %fusion) | data formatting | bytes 4194304 | tf_op jit(solution)/shard_map/reshape | solution.py:101
  (64 shorter events, 16.4 us)
Async XLA Ops:
  6.5 10.4 %copy-start = (f32[8,1,256,256]{3,2,1,0:T(8,128)S(1)}, f32[8,1,256,256]{3,2,1,0:T(8,128)}, u32[]{:S(2)}) copy-start(f32[8,1,256,256]{3,2,1,0:T(8,128)} %param.13) | copy-start | bytes 6291460
  6.5 63.1 %all-reduce.9.cloned.1.call-start = ((), (), s32[]{:S(2)}) async-start(), calls=%async_computation | async-start | bytes 524288 | tf_op jit(solution)/shard_map/psum | solution.py:24
  6.5 6.2 %copy-start.4 = (f32[8,1,256,1,256]{4,3,2,1,0:T(1,128)S(1)}, f32[8,1,256,1,256]{4,3,2,1,0:T(1,128)}, u32[]{:S(2)}) copy-start(f32[8,1,256,1,256]{4,3,2,1,0:T(1,128)} %param.9) | copy-start | bytes 6291460
  9.7 7.2 %copy-start.6 = (f32[8,1,256]{2,1,0:T(1,128)S(1)}, f32[8,1,256]{2,1,0:T(1,128)}, u32[]{:S(2)}) copy-start(f32[8,1,256]{2,1,0:T(1,128)} %param.14) | copy-start | bytes 24580
  9.7 7.6 %copy-start.7 = (f32[1,256,256]{2,1,0:T(8,128)S(1)}, f32[1,256,256]{2,1,0:T(8,128)}, u32[]{:S(2)}) copy-start(f32[1,256,256]{2,1,0:T(8,128)} %param.15) | copy-start | bytes 786436
  9.7 7.7 %copy-start.8 = (f32[1,256]{1,0:T(1,128)S(1)}, f32[1,256]{1,0:T(1,128)}, u32[]{:S(2)}) copy-start(f32[1,256]{1,0:T(1,128)} %param.17) | copy-start | bytes 3076
  9.7 54.5 %collective-permute-start.1 = (f32[8,256,256]{2,1,0:T(8,128)}, f32[8,256,256]{2,1,0:T(8,128)}, u32[]{:S(2)}, u32[]{:S(2)}) collective-permute-start(f32[8,256,256]{2,1,0:T(8,128)} %bitcast.125), channel_id=1, source_target_pairs={{0,16},{16,0},{1,17},{17,1},{2,18},{18,2},{3,19},{19,3},{4,20},{20... | collective-permute-start | bytes 6291464 | tf_op jit(solution)/shard_map/ppermute | solution.py:19
  14.3 4.9 copy-start.5
  14.3 55.4 %collective-permute-start = (f32[8,256,256]{2,1,0:T(8,128)}, f32[8,256,256]{2,1,0:T(8,128)}, u32[]{:S(2)}, u32[]{:S(2)}) collective-permute-start(f32[8,256,256]{2,1,0:T(8,128)} %bitcast.126), channel_id=1, source_target_pairs={{1,0},{2,1},{3,2},{4,3},{5,4},{6,5},{7,6},{8,7},{9,8},{10,9},{11,1... | collective-permute-start | bytes 6291464 | tf_op jit(solution)/shard_map/ppermute | solution.py:13
  20.2 132.9 %all-reduce.11.cloned.1.call-start = ((), (), s32[]{:S(2)}) async-start(), calls=%async_computation.1 | async-start | bytes 4194304 | tf_op jit(solution)/shard_map/psum | solution.py:97
  22.2 246.3 %all-reduce.15.cloned.1.call-start = ((), (), s32[]{:S(2)}) async-start(), calls=%async_computation.3 | async-start | bytes 4194304 | tf_op jit(solution)/shard_map/psum | solution.py:97
  160.4 1.4 copy-start.2
  166.8 126.6 %all-reduce.13.cloned.1.call-start = ((), (), s32[]{:S(2)}) async-start(), calls=%async_computation.2 | async-start | bytes 524288 | tf_op jit(solution)/shard_map/psum | solution.py:24
  166.9 144.6 %collective-permute-start.2 = (f32[8,256,256]{2,1,0:T(8,128)}, f32[8,256,256]{2,1,0:T(8,128)}, u32[]{:S(2)}, u32[]{:S(2)}) collective-permute-start(f32[8,256,256]{2,1,0:T(8,128)} %bitcast.126), channel_id=1, source_target_pairs={{0,1},{1,2},{2,3},{3,4},{4,5},{5,6},{6,7},{7,8},{8,9},{9,10},{10,1... | collective-permute-start | bytes 6291464 | tf_op jit(solution)/shard_map/ppermute | solution.py:13
  169.6 158.7 %all-reduce.17.cloned.1.call-start = ((), (), s32[]{:S(2)}) async-start(), calls=%async_computation.4 | async-start | bytes 524288 | tf_op jit(solution)/shard_map/psum | solution.py:24
  300.1 1.3 copy-start.1
  304.8 130.2 %all-reduce.19.cloned.1.call-start = ((), (), s32[]{:S(2)}) async-start(), calls=%async_computation.5 | async-start | bytes 4194304 | tf_op jit(solution)/shard_map/psum | solution.py:97
  306.5 239.9 %all-reduce.23.cloned.1.call-start = ((), (), s32[]{:S(2)}) async-start(), calls=%async_computation.7 | async-start | bytes 4194304 | tf_op jit(solution)/shard_map/psum | solution.py:97
  306.5 246.9 %collective-permute-start.3 = (f32[8,256,256]{2,1,0:T(8,128)}, f32[8,256,256]{2,1,0:T(8,128)}, u32[]{:S(2)}, u32[]{:S(2)}) collective-permute-start(f32[8,256,256]{2,1,0:T(8,128)} %bitcast.126), channel_id=1, source_target_pairs={{0,2},{1,3},{2,4},{3,5},{4,6},{5,7},{6,8},{7,9},{8,10},{9,11},{10,... | collective-permute-start | bytes 6291464 | tf_op jit(solution)/shard_map/ppermute | solution.py:13
  442.3 1.4 copy-start.3
  448.6 122.9 %all-reduce.21.cloned.1.call-start = ((), (), s32[]{:S(2)}) async-start(), calls=%async_computation.6 | async-start | bytes 524288 | tf_op jit(solution)/shard_map/psum | solution.py:24
Sparse Core Ops, SparseCore 0:
  20.4 31.0 all-reduce.8
  55.0 98.1 all-reduce.10
  166.9 101.5 all-reduce.14
  270.6 22.7 all-reduce.12
  305.0 23.2 all-reduce.16
  331.7 103.3 all-reduce.18
  448.7 97.6 all-reduce.22
  548.7 22.7 all-reduce.20
where the time goes:
time: 596 us; the launch traced here: 592 us
  waiting for transfers between devices  462 us (78%)
  matrix products  69 us (12%)
  local copies, waits for them, and re-layouts  22.5 us (4%)
  between operations  14.2 us (2%)
  starting transfers between devices  13.3 us (2%)
  other arithmetic  11.9 us (2%)
    psum x4, waiting for transfers between devices, body(): row_solved = lax.psum(slot_blocks, 'col')  373 us
    psum x4, waiting for transfers between devices, spread(): return lax.psum(jnp.where(mine, value, jnp.zeros_like(value)), axis)  52.6 us
    ppermute x1, waiting for transfers between devices, shifted(): return lax.ppermute(value, axis, pairs)  35.7 us
    dot_general x4, matrix products, body(): jnp.einsum('qab,qbc->qac', row_solved, moved_lower[offset], precision=EXACT)  28.6 us
    dot_general x4, matrix products, body(): jnp.einsum('qab,bc->qac', moved_upper[offset], column_block, precision=EX...  27.6 us
    unnamed x21, local copies, waits for them, and re-layouts  14.8 us
    dot_general x16, matrix products, matmul(): jnp.dot(former, latter, precision=EXACT, preferred_element_type=jnp.float32)  12.8 us
  transfers between devices with their start and end apart: 12, of which 8 were waited for; matrix products, arithmetic and copies ran while one was open for 12% of the time, Pallas kernels for 0%

commit v1 on v0

--- a/solution.py
+++ b/solution.py
@@ -94,7 +94,11 @@
         column_block = spread(solved, "row", jnp.remainder(target, row_count))
         upper_term = jnp.einsum("qab,bc->qac", moved_upper[offset], column_block, precision=EXACT)
         slot_blocks = jnp.where(on_front[:, None, None], solved[None], jnp.zeros_like(work))
-        row_solved = lax.psum(slot_blocks, "col")
+        row_solved = slot_blocks
+        for hop in (1, 2, 4, 8):
+            row_solved = row_solved + lax.ppermute(
+                row_solved, "col", [(dev, dev ^ hop) for dev in range(16)]
+            )
         lower_term = jnp.einsum("qab,qbc->qac", row_solved, moved_lower[offset], precision=EXACT)
         pending = col_pos - global_rows > offset
         work = jnp.where(pending[:, None, None], work - (upper_term + lower_term), work)

time: 596 us -> 849 us (1.42)
  waiting for transfers between devices: 462 us -> 699 us
  starting transfers between devices: 13.3 us -> 30.4 us
    ppermute x0 -> x16, waiting for transfers between devices: none -> 617 us  [body(): lax.ppermute(row_solved, 'col', [(dev, dev ^ hop) for dev in range(16)])]
    psum x4 -> x0, waiting for transfers between devices: 373 us -> none  [body(): row_solved = lax.psum(slot_blocks, 'col')]
    ppermute x1, waiting for transfers between devices: 35.7 us -> 0.01 us  [shifted(): return lax.ppermute(value, axis, pairs)]
    psum x4, waiting for transfers between devices: 52.6 us -> 81.8 us  [spread(): return lax.psum(jnp.where(mine, value, jnp.zeros_like(value)), axis)]
    ppermute x0 -> x16, starting transfers between devices: none -> 18.9 us  [body(): lax.ppermute(row_solved, 'col', [(dev, dev ^ hop) for dev in range(16)])]
    add x0 -> x12, other arithmetic: none -> 9.12 us  [body(): row_solved + lax.ppermute(row_solved, 'col', [(dev, dev ^ hop) for dev in...]
  transfers between devices with their start and end apart: 12 -> 24, of which waited for: 8 -> 20; matrix products, arithmetic and copies ran while one was open for 12% -> 5% of each run, Pallas kernels for 0% -> 0%
where the time goes in v1:
time: 849 us; the launch traced here: 845 us
  waiting for transfers between devices  699 us (82%)
  matrix products  63.9 us (8%)
  starting transfers between devices  30.4 us (4%)
  local copies, waits for them, and re-layouts  22.2 us (3%)
  other arithmetic  15.4 us (2%)
  between operations  14 us (2%)
    ppermute x16, waiting for transfers between devices, body(): lax.ppermute(row_solved, 'col', [(dev, dev ^ hop) for dev in range(16)])  617 us
    psum x4, waiting for transfers between devices, spread(): return lax.psum(jnp.where(mine, value, jnp.zeros_like(value)), axis)  81.8 us
    dot_general x4, matrix products, body(): jnp.einsum('qab,qbc->qac', row_solved, moved_lower[offset], precision=EXACT)  28.9 us
    dot_general x4, matrix products, body(): jnp.einsum('qab,bc->qac', moved_upper[offset], column_block, precision=EX...  21.2 us
    ppermute x16, starting transfers between devices, body(): lax.ppermute(row_solved, 'col', [(dev, dev ^ hop) for dev in range(16)])  18.9 us
  transfers between devices with their start and end apart: 24, of which 20 were waited for; matrix products, arithmetic and copies ran while one was open for 5% of the time, Pallas kernels for 0%

profile of v1, /device:TPU:0, one launch (start us, length us, event | category | flops | bytes accessed | tf_op | source)
XLA Modules:
  0.0 845.1 jit_solution(7122548077572016746)
XLA Ops:
  14.1 3.8 collective-permute-done.1
  21.2 45.9 %collective-permute-done.2 = f32[8,256,256]{1,2,0:T(8,128)S(1)} collective-permute-done((f32[8,256,256]{1,2,0:T(8,128)S(1)}, f32[8,256,256]{1,2,0:T(8,128)S(1)}, u32[]{:S(2)}, u32[]{:S(2)}) %collective-permute-start.2) | collective-permute-done | bytes 2097184 | tf_op jit(solution)/shard_map/ppermute | solution.py:99
  75.2 39.4 %collective-permute-done.3 = f32[8,256,256]{1,2,0:T(8,128)S(1)} collective-permute-done((f32[8,256,256]{1,2,0:T(8,128)S(1)}, f32[8,256,256]{1,2,0:T(8,128)S(1)}, u32[]{:S(2)}, u32[]{:S(2)}) %collective-permute-start.3) | collective-permute-done | bytes 2097184 | tf_op jit(solution)/shard_map/ppermute | solution.py:99
  119.2 6.1 copy.11
  125.3 5.3 pad_maximum_fusion
  130.5 10.9 %all-reduce.5.cloned.1.call-done = f32[256,256]{1,0:T(8,128)} async-done(((f32[256,256]{1,0:T(8,128)}), f32[256,256]{1,0:T(8,128)}) %all-reduce.5.cloned.1.call-update) | async-done | bytes 262160 | tf_op jit(solution)/shard_map/psum | solution.py:24
  141.4 5.3 fusion.36
  146.8 62.0 %collective-permute-done.4 = f32[8,256,256]{1,2,0:T(8,128)} collective-permute-done((f32[8,256,256]{1,2,0:T(8,128)}, f32[8,256,256]{1,2,0:T(8,128)}, u32[]{:S(2)}, u32[]{:S(2)}) %collective-permute-start.4) | collective-permute-done | bytes 2097184 | tf_op jit(solution)/shard_map/ppermute | solution.py:99
  208.7 6.9 subtract_select_fusion.3
  220.7 4.1 collective-permute-done.6
  226.4 46.5 %collective-permute-done.7 = f32[8,256,256]{1,2,0:T(8,128)S(1)} collective-permute-done((f32[8,256,256]{1,2,0:T(8,128)S(1)}, f32[8,256,256]{1,2,0:T(8,128)S(1)}, u32[]{:S(2)}, u32[]{:S(2)}) %collective-permute-start.7) | collective-permute-done | bytes 2097184 | tf_op jit(solution)/shard_map/ppermute | solution.py:99
  273.6 46.5 %collective-permute-done.8 = f32[8,256,256]{1,2,0:T(8,128)S(1)} collective-permute-done((f32[8,256,256]{1,2,0:T(8,128)S(1)}, f32[8,256,256]{1,2,0:T(8,128)S(1)}, u32[]{:S(2)}, u32[]{:S(2)}) %collective-permute-start.8) | collective-permute-done | bytes 2097184 | tf_op jit(solution)/shard_map/ppermute | solution.py:99
  324.4 22.2 %all-reduce.7.cloned.1.call-done = f32[256,256]{1,0:T(8,128)} async-done(((f32[256,256]{1,0:T(8,128)}), f32[256,256]{1,0:T(8,128)}) %all-reduce.7.cloned.1.call-update) | async-done | bytes 262160 | tf_op jit(solution)/shard_map/psum | solution.py:24
  346.6 5.3 fusion.32
  351.9 62.0 %collective-permute-done.9 = f32[8,256,256]{1,2,0:T(8,128)} collective-permute-done((f32[8,256,256]{1,2,0:T(8,128)}, f32[8,256,256]{1,2,0:T(8,128)}, u32[]{:S(2)}, u32[]{:S(2)}) %collective-permute-start.9) | collective-permute-done | bytes 2097184 | tf_op jit(solution)/shard_map/ppermute | solution.py:99
  413.9 6.9 subtract_select_fusion.2
  425.8 4.1 collective-permute-done.11
  431.5 46.5 %collective-permute-done.12 = f32[8,256,256]{1,2,0:T(8,128)S(1)} collective-permute-done((f32[8,256,256]{1,2,0:T(8,128)S(1)}, f32[8,256,256]{1,2,0:T(8,128)S(1)}, u32[]{:S(2)}, u32[]{:S(2)}) %collective-permute-start.12) | collective-permute-done | bytes 2097184 | tf_op jit(solution)/shard_map/ppermute | solution.py:99
  481.4 43.8 %collective-permute-done.13 = f32[8,256,256]{1,2,0:T(8,128)S(1)} collective-permute-done((f32[8,256,256]{1,2,0:T(8,128)S(1)}, f32[8,256,256]{1,2,0:T(8,128)S(1)}, u32[]{:S(2)}, u32[]{:S(2)}) %collective-permute-start.13) | collective-permute-done | bytes 2097184 | tf_op jit(solution)/shard_map/ppermute | solution.py:99
  529.2 24.2 %all-reduce.9.cloned.1.call-done = f32[256,256]{1,0:T(8,128)} async-done(((f32[256,256]{1,0:T(8,128)}), f32[256,256]{1,0:T(8,128)}) %all-reduce.9.cloned.1.call-update) | async-done | bytes 262160 | tf_op jit(solution)/shard_map/psum | solution.py:24
  553.4 5.3 fusion.28
  558.7 60.3 %collective-permute-done.14 = f32[8,256,256]{1,2,0:T(8,128)} collective-permute-done((f32[8,256,256]{1,2,0:T(8,128)}, f32[8,256,256]{1,2,0:T(8,128)}, u32[]{:S(2)}, u32[]{:S(2)}) %collective-permute-start.14) | collective-permute-done | bytes 2097184 | tf_op jit(solution)/shard_map/ppermute | solution.py:99
  619.0 6.9 subtract_select_fusion.1
  630.9 4.1 collective-permute-done.16
  636.6 46.5 %collective-permute-done.17 = f32[8,256,256]{1,2,0:T(8,128)S(1)} collective-permute-done((f32[8,256,256]{1,2,0:T(8,128)S(1)}, f32[8,256,256]{1,2,0:T(8,128)S(1)}, u32[]{:S(2)}, u32[]{:S(2)}) %collective-permute-start.17) | collective-permute-done | bytes 2097184 | tf_op jit(solution)/shard_map/ppermute | solution.py:99
  683.9 5.0 collective-permute-start.15
  688.8 41.5 %collective-permute-done.18 = f32[8,256,256]{1,2,0:T(8,128)S(1)} collective-permute-done((f32[8,256,256]{1,2,0:T(8,128)S(1)}, f32[8,256,256]{1,2,0:T(8,128)S(1)}, u32[]{:S(2)}, u32[]{:S(2)}) %collective-permute-start.18) | collective-permute-done | bytes 2097184 | tf_op jit(solution)/shard_map/ppermute | solution.py:99
  734.0 24.5 %all-reduce.11.cloned.1.call-done = f32[256,256]{1,0:T(8,128)} async-done(((f32[256,256]{1,0:T(8,128)}), f32[256,256]{1,0:T(8,128)}) %all-reduce.11.cloned.1.call-update) | async-done | bytes 262160 | tf_op jit(solution)/shard_map/psum | solution.py:24
  758.5 5.3 fusion.24
  763.8 60.3 %collective-permute-done.19 = f32[8,256,256]{1,2,0:T(8,128)} collective-permute-done((f32[8,256,256]{1,2,0:T(8,128)}, f32[8,256,256]{1,2,0:T(8,128)}, u32[]{:S(2)}, u32[]{:S(2)}) %collective-permute-start.19) | collective-permute-done | bytes 2097184 | tf_op jit(solution)/shard_map/ppermute | solution.py:99
  824.1 8.2 fusion
  832.3 6.0 copy.27
  (104 shorter events, 59.5 us)
Async XLA Ops:
  6.5 5.6 copy-start.9
  6.5 134.9 %all-reduce.5.cloned.1.call-start = ((), (), s32[]{:S(2)}) async-start(), calls=%async_computation | async-start | bytes 524288 | tf_op jit(solution)/shard_map/psum | solution.py:24
  13.6 4.3 collective-permute-start.1
  18.2 51.1 %copy-start.10 = (f32[8,1,256,1,256]{4,3,2,1,0:T(1,128)S(1)}, f32[8,1,256,1,256]{4,3,2,1,0:T(1,128)}, u32[]{:S(2)}) copy-start(f32[8,1,256,1,256]{4,3,2,1,0:T(1,128)} %param.10) | copy-start | bytes 6291460
  18.2 48.8 %collective-permute-start.2 = (f32[8,256,256]{1,2,0:T(8,128)S(1)}, f32[8,256,256]{1,2,0:T(8,128)S(1)}, u32[]{:S(2)}, u32[]{:S(2)}) collective-permute-start(f32[8,256,256]{1,2,0:T(8,128)S(1)} %fusion.17), channel_id=1, source_target_pairs={{0,2},{1,3},{2,0},{3,1},{4,6},{5,7},{6,4},{7,5},{8,10},{9,11},{10,... | collective-permute-start | bytes 6291464 | tf_op jit(solution)/shard_map/ppermute | solution.py:99
  67.5 47.2 %collective-permute-start.3 = (f32[8,256,256]{1,2,0:T(8,128)S(1)}, f32[8,256,256]{1,2,0:T(8,128)S(1)}, u32[]{:S(2)}, u32[]{:S(2)}) collective-permute-start(f32[8,256,256]{1,2,0:T(8,128)S(1)} %fusion.115), channel_id=1, source_target_pairs={{0,4},{1,5},{2,6},{3,7},{4,0},{5,1},{6,2},{7,3},{8,12},{9,13},{10,... | collective-permute-start | bytes 6291464 | tf_op jit(solution)/shard_map/ppermute | solution.py:99
  70.9 54.4 %collective-permute-start.5 = (f32[8,256,256]{2,1,0:T(8,128)}, f32[8,256,256]{2,1,0:T(8,128)}, u32[]{:S(2)}, u32[]{:S(2)}) collective-permute-start(f32[8,256,256]{2,1,0:T(8,128)} %bitcast.121), channel_id=1, source_target_pairs={{0,16},{16,0},{1,17},{17,1},{2,18},{18,2},{3,19},{19,3},{4,20},{20... | collective-permute-start | bytes 6291464 | tf_op jit(solution)/shard_map/ppermute | solution.py:19
  73.9 67.5 %collective-permute-start = (f32[8,256,256]{2,1,0:T(8,128)}, f32[8,256,256]{2,1,0:T(8,128)}, u32[]{:S(2)}, u32[]{:S(2)}) collective-permute-start(f32[8,256,256]{2,1,0:T(8,128)} %bitcast.122), channel_id=1, source_target_pairs={{1,0},{2,1},{3,2},{4,3},{5,4},{6,5},{7,6},{8,7},{9,8},{10,9},{11,1... | collective-permute-start | bytes 6291464 | tf_op jit(solution)/shard_map/ppermute | solution.py:13
  116.2 92.5 %collective-permute-start.4 = (f32[8,256,256]{1,2,0:T(8,128)}, f32[8,256,256]{1,2,0:T(8,128)}, u32[]{:S(2)}, u32[]{:S(2)}) collective-permute-start(f32[8,256,256]{1,2,0:T(8,128)} %add.252), channel_id=1, source_target_pairs={{0,8},{1,9},{2,10},{3,11},{4,12},{5,13},{6,14},{7,15},{8,0},{9,1},... | collective-permute-start | bytes 6291464 | tf_op jit(solution)/shard_map/ppermute | solution.py:99
  118.8 227.8 %all-reduce.7.cloned.1.call-start = ((), (), s32[]{:S(2)}) async-start(), calls=%async_computation.1 | async-start | bytes 524288 | tf_op jit(solution)/shard_map/psum | solution.py:24
  141.4 67.3 %copy-start.3 = (f32[10,256,256]{2,1,0:T(8,128)S(1)}, f32[10,256,256]{2,1,0:T(8,128)}, u32[]{:S(2)}) copy-start(f32[10,256,256]{2,1,0:T(8,128)} %get-tuple-element.8) | copy-start | bytes 7864324
  208.7 8.7 %copy-start.11 = (f32[1,256,256]{2,1,0:T(8,128)S(1)}, f32[1,256,256]{2,1,0:T(8,128)}, u32[]{:S(2)}) copy-start(f32[1,256,256]{2,1,0:T(8,128)} %param.15) | copy-start | bytes 786436
  208.7 8.7 %copy-start.12 = (f32[1,256]{1,0:T(1,128)S(1)}, f32[1,256]{1,0:T(1,128)}, u32[]{:S(2)}) copy-start(f32[1,256]{1,0:T(1,128)} %param.17) | copy-start | bytes 3076
  220.6 4.2 collective-permute-start.6
  225.1 47.7 %collective-permute-start.7 = (f32[8,256,256]{1,2,0:T(8,128)S(1)}, f32[8,256,256]{1,2,0:T(8,128)S(1)}, u32[]{:S(2)}, u32[]{:S(2)}) collective-permute-start(f32[8,256,256]{1,2,0:T(8,128)S(1)} %fusion.18), channel_id=1, source_target_pairs={{0,2},{1,3},{2,0},{3,1},{4,6},{5,7},{6,4},{7,5},{8,10},{9,11},{10,... | collective-permute-start | bytes 6291464 | tf_op jit(solution)/shard_map/ppermute | solution.py:99
  273.2 46.9 %collective-permute-start.8 = (f32[8,256,256]{1,2,0:T(8,128)S(1)}, f32[8,256,256]{1,2,0:T(8,128)S(1)}, u32[]{:S(2)}, u32[]{:S(2)}) collective-permute-start(f32[8,256,256]{1,2,0:T(8,128)S(1)} %fusion.114), channel_id=1, source_target_pairs={{0,4},{1,5},{2,6},{3,7},{4,0},{5,1},{6,2},{7,3},{8,12},{9,13},{10,... | collective-permute-start | bytes 6291464 | tf_op jit(solution)/shard_map/ppermute | solution.py:99
  321.8 92.1 %collective-permute-start.9 = (f32[8,256,256]{1,2,0:T(8,128)}, f32[8,256,256]{1,2,0:T(8,128)}, u32[]{:S(2)}, u32[]{:S(2)}) collective-permute-start(f32[8,256,256]{1,2,0:T(8,128)} %add.264), channel_id=1, source_target_pairs={{0,8},{1,9},{2,10},{3,11},{4,12},{5,13},{6,14},{7,15},{8,0},{9,1},... | collective-permute-start | bytes 6291464 | tf_op jit(solution)/shard_map/ppermute | solution.py:99
  323.8 229.6 %all-reduce.9.cloned.1.call-start = ((), (), s32[]{:S(2)}) async-start(), calls=%async_computation.2 | async-start | bytes 524288 | tf_op jit(solution)/shard_map/psum | solution.py:24
  346.6 67.3 %copy-start.1 = (f32[10,256,256]{2,1,0:T(8,128)S(1)}, f32[10,256,256]{2,1,0:T(8,128)}, u32[]{:S(2)}) copy-start(f32[10,256,256]{2,1,0:T(8,128)} %get-tuple-element.7) | copy-start | bytes 7864324
  425.7 4.2 collective-permute-start.11
  430.2 47.7 %collective-permute-start.12 = (f32[8,256,256]{1,2,0:T(8,128)S(1)}, f32[8,256,256]{1,2,0:T(8,128)S(1)}, u32[]{:S(2)}, u32[]{:S(2)}) collective-permute-start(f32[8,256,256]{1,2,0:T(8,128)S(1)} %fusion.19), channel_id=1, source_target_pairs={{0,2},{1,3},{2,0},{3,1},{4,6},{5,7},{6,4},{7,5},{8,10},{9,11},{10,... | collective-permute-start | bytes 6291464 | tf_op jit(solution)/shard_map/ppermute | solution.py:99
  478.3 46.9 %collective-permute-start.13 = (f32[8,256,256]{1,2,0:T(8,128)S(1)}, f32[8,256,256]{1,2,0:T(8,128)S(1)}, u32[]{:S(2)}, u32[]{:S(2)}) collective-permute-start(f32[8,256,256]{1,2,0:T(8,128)S(1)} %fusion.113), channel_id=1, source_target_pairs={{0,4},{1,5},{2,6},{3,7},{4,0},{5,1},{6,2},{7,3},{8,12},{9,13},{10,... | collective-permute-start | bytes 6291464 | tf_op jit(solution)/shard_map/ppermute | solution.py:99
  478.7 50.4 %collective-permute-start.10 = (f32[8,256,256]{2,1,0:T(8,128)}, f32[8,256,256]{2,1,0:T(8,128)}, u32[]{:S(2)}, u32[]{:S(2)}) collective-permute-start(f32[8,256,256]{2,1,0:T(8,128)} %bitcast.122), channel_id=1, source_target_pairs={{0,1},{1,2},{2,3},{3,4},{4,5},{5,6},{6,7},{7,8},{8,9},{9,10},{10,1... | collective-permute-start | bytes 6291464 | tf_op jit(solution)/shard_map/ppermute | solution.py:13
  526.9 92.1 %collective-permute-start.14 = (f32[8,256,256]{1,2,0:T(8,128)}, f32[8,256,256]{1,2,0:T(8,128)}, u32[]{:S(2)}, u32[]{:S(2)}) collective-permute-start(f32[8,256,256]{1,2,0:T(8,128)} %add.275), channel_id=1, source_target_pairs={{0,8},{1,9},{2,10},{3,11},{4,12},{5,13},{6,14},{7,15},{8,0},{9,1},... | collective-permute-start | bytes 6291464 | tf_op jit(solution)/shard_map/ppermute | solution.py:99
  528.9 229.6 %all-reduce.11.cloned.1.call-start = ((), (), s32[]{:S(2)}) async-start(), calls=%async_computation.3 | async-start | bytes 524288 | tf_op jit(solution)/shard_map/psum | solution.py:24
  553.4 65.6 %copy-start.4 = (f32[10,256,256]{2,1,0:T(8,128)S(1)}, f32[10,256,256]{2,1,0:T(8,128)}, u32[]{:S(2)}) copy-start(f32[10,256,256]{2,1,0:T(8,128)} %get-tuple-element.8) | copy-start | bytes 7864324
  630.8 4.2 collective-permute-start.16
  635.4 47.7 %collective-permute-start.17 = (f32[8,256,256]{1,2,0:T(8,128)S(1)}, f32[8,256,256]{1,2,0:T(8,128)S(1)}, u32[]{:S(2)}, u32[]{:S(2)}) collective-permute-start(f32[8,256,256]{1,2,0:T(8,128)S(1)} %fusion.20), channel_id=1, source_target_pairs={{0,2},{1,3},{2,0},{3,1},{4,6},{5,7},{6,4},{7,5},{8,10},{9,11},{10,... | collective-permute-start | bytes 6291464 | tf_op jit(solution)/shard_map/ppermute | solution.py:99
  683.5 46.9 %collective-permute-start.18 = (f32[8,256,256]{1,2,0:T(8,128)S(1)}, f32[8,256,256]{1,2,0:T(8,128)S(1)}, u32[]{:S(2)}, u32[]{:S(2)}) collective-permute-start(f32[8,256,256]{1,2,0:T(8,128)S(1)} %fusion.112), channel_id=1, source_target_pairs={{0,4},{1,5},{2,6},{3,7},{4,0},{5,1},{6,2},{7,3},{8,12},{9,13},{10,... | collective-permute-start | bytes 6291464 | tf_op jit(solution)/shard_map/ppermute | solution.py:99
  683.9 50.1 %collective-permute-start.15 = (f32[8,256,256]{2,1,0:T(8,128)}, f32[8,256,256]{2,1,0:T(8,128)}, u32[]{:S(2)}, u32[]{:S(2)}) collective-permute-start(f32[8,256,256]{2,1,0:T(8,128)} %bitcast.122), channel_id=1, source_target_pairs={{0,2},{1,3},{2,4},{3,5},{4,6},{5,7},{6,8},{7,9},{8,10},{9,11},{10,... | collective-permute-start | bytes 6291464 | tf_op jit(solution)/shard_map/ppermute | solution.py:13
  732.0 92.1 %collective-permute-start.19 = (f32[8,256,256]{1,2,0:T(8,128)}, f32[8,256,256]{1,2,0:T(8,128)}, u32[]{:S(2)}, u32[]{:S(2)}) collective-permute-start(f32[8,256,256]{1,2,0:T(8,128)} %add.287), channel_id=1, source_target_pairs={{0,8},{1,9},{2,10},{3,11},{4,12},{5,13},{6,14},{7,15},{8,0},{9,1},... | collective-permute-start | bytes 6291464 | tf_op jit(solution)/shard_map/ppermute | solution.py:99
  758.5 65.6 %copy-start.2 = (f32[10,256,256]{2,1,0:T(8,128)S(1)}, f32[10,256,256]{2,1,0:T(8,128)}, u32[]{:S(2)}) copy-start(f32[10,256,256]{2,1,0:T(8,128)} %get-tuple-element.7) | copy-start | bytes 7864324
  (5 other events, 10.6 us)
Sparse Core Ops, SparseCore 0:
  118.9 22.5 all-reduce.4
  323.9 22.6 all-reduce.6
  529.0 24.3 all-reduce.8
  734.1 24.3 all-reduce.10
